TPU v7x, 32 devices: a whole 2x2x4 slice. The times are simulated.
32 devices in a mesh: rep: 2 (over x), dp: 16 (over y, z, core).
Axes of the slice: x: 2, y: 2, z: 4, core: 2. Of those that a mesh axis runs over, the one named last changes fastest.
Arguments:
- g_w_gate: bfloat16 [32, 2, 1152, 4608], P(('rep', 'dp')), parts along dimension 0
- g_w_up: bfloat16 [32, 2, 1152, 4608], P(('rep', 'dp')), parts along dimension 0
- g_w_down: bfloat16 [32, 2, 4608, 1152], P(('rep', 'dp')), parts along dimension 0
- w_gate: bfloat16 [2, 1152, 4608], replicated
- w_up: bfloat16 [2, 1152, 4608], replicated
- w_down: bfloat16 [2, 4608, 1152], replicated
- m_w_gate: float32 [2, 1152, 4608], P(None, 'dp')
- m_w_up: float32 [2, 1152, 4608], P(None, 'dp')
- m_w_down: float32 [2, 4608, 1152], P(None, 'dp')
- v_w_gate: float32 [2, 1152, 4608], P(None, 'dp')
- v_w_up: float32 [2, 1152, 4608], P(None, 'dp')
- v_w_down: float32 [2, 4608, 1152], P(None, 'dp')
Outputs:
- output 1: bfloat16 [4, 1152, 4608], P('rep'), parts along dimension 0
- output 2: bfloat16 [4, 1152, 4608], P('rep'), parts along dimension 0
- output 3: bfloat16 [4, 4608, 1152], P('rep'), parts along dimension 0
- output 4: float32 [4, 1152, 4608], P('rep', 'dp'), parts along dimension 0
- output 5: float32 [4, 1152, 4608], P('rep', 'dp'), parts along dimension 0
- output 6: float32 [4, 4608, 1152], P('rep', 'dp'), parts along dimension 0
- output 7: float32 [4, 1152, 4608], P('rep', 'dp'), parts along dimension 0
- output 8: float32 [4, 1152, 4608], P('rep', 'dp'), parts along dimension 0
- output 9: float32 [4, 4608, 1152], P('rep', 'dp'), parts along dimension 0
There are 2 independent parts. A program takes and returns all parts, laid end to end along the dimension named above; an argument that names none is the same for every part.
All inputs are finite; a program needn't handle non-finite values.
Results may differ from a plain program's by a relative error of at most 0.022.
Values are sent between devices in bfloat16 or wider.
A program may use at most 2 GiB of HBM per device.

v0:
```python
import jax
import jax.numpy as jnp
from jax import lax
from jax.sharding import PartitionSpec as P


def adamw(w, m, v, g):
    m = 0.9 * m + 0.1 * g
    v = 0.95 * v + 0.05 * g * g
    step = m * lax.rsqrt(v + 1e-8) + 0.1 * w
    return (w - 0.02 * step).astype(jnp.bfloat16), m, v


def solution(mesh):
    def step(*arrays):
        terms, weights, m, v = (arrays[i : i + 3] for i in (0, 3, 6, 9))
        gradients = [lax.psum_scatter(t[0], "dp", scatter_dimension=1, tiled=True).astype(jnp.float32) for t in terms]
        me = lax.axis_index("dp")
        own = [lax.dynamic_slice_in_dim(w, me * one.shape[1], one.shape[1], 1).astype(jnp.float32) for w, one in zip(weights, m, strict=True)]
        new = [adamw(w, m, v, g) for w, m, v, g in zip(own, m, v, gradients, strict=True)]
        whole = [lax.all_gather(one[0], "dp", axis=1, tiled=True) for one in new]
        return (*whole, *(one[1] for one in new), *(one[2] for one in new))

    all_of, cut = P(None, None, None), P(None, "dp", None)
    return jax.shard_map(
        step,
        mesh=mesh,
        in_specs=(P(("rep", "dp"), None, None, None),) * 3 + (all_of,) * 3 + (cut,) * 6,
        out_specs=(P("rep", None, None),) * 3 + (P("rep", "dp", None),) * 6,
        check_vma=False,
    )
```

profile of v0, /device:TPU:0, one launch (start us, length us, event | category | flops | bytes accessed | tf_op | source)
XLA Modules:
  0.0 1037.8 jit_solution(6283881227875384947)
XLA Ops:
  7.2 0.0 reduce-scatter.8.cloned.1.call-start
  7.2 0.7 reduce-scatter.8.cloned.1.call-update
  7.9 0.0 reduce-scatter.10.cloned.1.call-start
  8.0 102.6 %copy.21 = bf16[2,1152,4608]{2,0,1:T(2,128)(2,1)S(1)} copy(bf16[2,1152,4608]{2,1,0:T(8,128)(2,1)} %bitcast.15) | data formatting | bytes 42467328
  110.6 7.8 copy.25
  118.3 0.0 reduce-scatter.10.cloned.1.call-update
  118.4 0.0 reduce-scatter.12.cloned.1.call-start
  118.4 102.6 %copy.23 = bf16[2,1152,4608]{2,0,1:T(2,128)(2,1)S(1)} copy(bf16[2,1152,4608]{2,1,0:T(8,128)(2,1)} %bitcast.16) | data formatting | bytes 42467328
  221.0 7.8 copy.26
  228.8 0.0 reduce-scatter.12.cloned.1.call-update
  228.8 0.0 all-gather.8.cloned.1.call-start
  228.9 0.0 reduce-scatter.8.cloned.1.call-done
  228.9 1.6 copy-done.1
  230.6 6.1 fusion.10
  236.7 0.0 all-gather.8.cloned.1.call-update
  236.7 0.0 all-gather.4.cloned.1.call-start
  236.7 202.4 %reduce-scatter.10.cloned.1.call-done = bf16[72,9216]{1,0:T(8,128)(2,1)} async-done(((bf16[1152,9216]{1,0:T(8,128)(2,1)}), bf16[72,9216]{1,0:T(8,128)(2,1)}) %reduce-scatter.10.cloned.1.call-update) | async-done | bytes 1327120
  439.1 3.6 reshape.19
  442.8 6.5 fusion.2
  449.3 0.0 all-gather.4.cloned.1.call-update
  449.3 0.2 all-gather.6.cloned.1.call-start
  449.5 203.8 %reduce-scatter.12.cloned.1.call-done = bf16[72,9216]{1,0:T(8,128)(2,1)} async-done(((bf16[1152,9216]{1,0:T(8,128)(2,1)}), bf16[72,9216]{1,0:T(8,128)(2,1)}) %reduce-scatter.12.cloned.1.call-update) | async-done | bytes 1327120
  653.3 3.6 reshape.21
  656.9 6.5 fusion.6
  663.5 101.1 %all-gather.8.cloned.1.call-done = bf16[2,4608,1152]{2,1,0:T(8,128)(2,1)} async-done(((bf16[2,288,1152]{2,1,0:T(8,128)(2,1)}), bf16[2,4608,1152]{2,1,0:T(8,128)(2,1)}) %all-gather.8.cloned.1.call-update) | async-done | bytes 21233680 | tf_op jit(solution)/shard_map/all_gather | solution.py:21
  764.5 111.9 %all-gather.4.cloned.1.call-done = bf16[2,1152,4608]{2,1,0:T(8,128)(2,1)} async-done(((bf16[2,72,4608]{2,1,0:T(8,128)(2,1)}), bf16[2,1152,4608]{2,1,0:T(8,128)(2,1)}) %all-gather.4.cloned.1.call-update) | async-done | bytes 21233680 | tf_op jit(solution)/shard_map/all_gather | solution.py:21
  876.4 111.9 %all-gather.6.cloned.1.call-done = bf16[2,1152,4608]{2,1,0:T(8,128)(2,1)} async-done(((bf16[2,72,4608]{2,1,0:T(8,128)(2,1)}), bf16[2,1152,4608]{2,1,0:T(8,128)(2,1)}) %all-gather.6.cloned.1.call-update) | async-done | bytes 21233680 | tf_op jit(solution)/shard_map/all_gather | solution.py:21
  988.4 21.0 %copy.38 = bf16[2,1152,4608]{2,1,0:T(8,128)(2,1)} copy(bf16[2,1152,4608]{2,1,0:T(8,128)(2,1)} %all-gather.4.cloned.1.call-done) | data formatting | bytes 42467328
  1009.4 10.8 %copy.39 = bf16[2,1152,4608]{2,1,0:T(8,128)(2,1)} copy(bf16[2,1152,4608]{2,1,0:T(8,128)(2,1)S(1)} %copy-done) | data formatting | bytes 42467328
  1020.1 1.8 slice-done.3
  1021.9 1.4 slice-done.4
  1023.3 7.6 copy.40
  (15 shorter events, 0.0 us)
Async XLA Ops:
  7.2 221.7 %reduce-scatter.8.cloned.1.call-start = ((), (), s32[]{:S(2)}) async-start(), calls=%async_computation.5 | async-start | bytes 22560768 | tf_op jit(solution)/shard_map/reduce_scatter | solution.py:17
  7.9 431.2 %reduce-scatter.10.cloned.1.call-start = ((), (), s32[]{:S(2)}) async-start(), calls=%async_computation.7 | async-start | bytes 22560768
  118.4 535.0 %reduce-scatter.12.cloned.1.call-start = ((), (), s32[]{:S(2)}) async-start(), calls=%async_computation.8 | async-start | bytes 22560768
  228.8 1.8 copy-start.1
  228.8 535.7 %all-gather.8.cloned.1.call-start = ((), (), s32[]{:S(2)}) async-start(), calls=%async_computation.6 | async-start | bytes 22560768 | tf_op jit(solution)/shard_map/all_gather | solution.py:21
  236.7 639.8 %all-gather.4.cloned.1.call-start = ((), (), s32[]{:S(2)}) async-start(), calls=%async_computation.3 | async-start | bytes 22560768 | tf_op jit(solution)/shard_map/all_gather | solution.py:21
  449.3 539.0 %all-gather.6.cloned.1.call-start = ((), (), s32[]{:S(2)}) async-start(), calls=%async_computation.4 | async-start | bytes 22560768 | tf_op jit(solution)/shard_map/all_gather | solution.py:21
  988.3 21.0 %copy-start = (bf16[2,1152,4608]{2,1,0:T(8,128)(2,1)S(1)}, bf16[2,1152,4608]{2,1,0:T(8,128)(2,1)}, u32[]{:S(2)}) copy-start(bf16[2,1152,4608]{2,1,0:T(8,128)(2,1)} %all-gather.6.cloned.1.call-done) | copy-start | bytes 63700996
  988.3 31.8 %slice-start = ((s8[21233664]{0:T(1024)(128)(4,1)}), s8[4194304]{0:T(1024)(128)(4,1)S(1)}, s32[]{:S(2)}) async-start(s8[21233664]{0:T(1024)(128)(4,1)} %bitcast.18), calls=%async_computation.9 | async-start | bytes 8388608
  988.3 31.8 %slice-start.1 = ((s8[21233664]{0:T(1024)(128)(4,1)}), s8[4194304]{0:T(1024)(128)(4,1)S(1)}, s32[]{:S(2)}) async-start(s8[21233664]{0:T(1024)(128)(4,1)} %bitcast.18), calls=%async_computation.10 | async-start | bytes 8388608
  988.3 31.8 %slice-start.2 = ((s8[21233664]{0:T(1024)(128)(4,1)}), s8[4194304]{0:T(1024)(128)(4,1)S(1)}, s32[]{:S(2)}) async-start(s8[21233664]{0:T(1024)(128)(4,1)} %bitcast.18), calls=%async_computation.11 | async-start | bytes 8388608
  988.4 33.5 %slice-start.3 = ((s8[21233664]{0:T(1024)(128)(4,1)}), s8[4194304]{0:T(1024)(128)(4,1)S(1)}, s32[]{:S(2)}) async-start(s8[21233664]{0:T(1024)(128)(4,1)} %bitcast.18), calls=%async_computation.12 | async-start | bytes 8388608
  1009.3 13.9 %slice-start.4 = ((s8[21233664]{0:T(1024)(128)(4,1)}), s8[4194304]{0:T(1024)(128)(4,1)S(1)}, s32[]{:S(2)}) async-start(s8[21233664]{0:T(1024)(128)(4,1)} %bitcast.18), calls=%async_computation.13 | async-start | bytes 8388608
  1009.3 13.9 %slice-start.5 = ((s8[21233664]{0:T(1024)(128)(4,1)}), s8[262144]{0:T(1024)(128)(4,1)S(1)}, s32[]{:S(2)}) async-start(s8[21233664]{0:T(1024)(128)(4,1)} %bitcast.18), calls=%async_computation.14 | async-start | bytes 524288
Sparse Core Ops, SparseCore 0:
  12.1 212.8 reduce-scatter.7
  229.7 209.3 reduce-scatter.9
  443.8 209.4 reduce-scatter.11
  655.3 109.1 all-gather.7
  766.5 109.8 all-gather.3
  878.4 109.8 all-gather.5
where the time goes:
time: 1040 us
  waiting for transfers between devices  732 us (70%)
  local copies, waits for them, and re-layouts  272 us (26%)
  other arithmetic  19.1 us (2%)
  between operations  14.2 us (1%)
    unnamed x8, waiting for transfers between devices  407 us
    all_gather x3, waiting for transfers between devices, step(): whole = [lax.all_gather(one[0], 'dp', axis=1, tiled=True) for one in new]  325 us
    unnamed x25, local copies, waits for them, and re-layouts  272 us
  transfers between devices with their start and end apart: 6, of which 5 were waited for; matrix products, arithmetic and copies ran while one was open for 24% of the time, Pallas kernels for 0%

commit v1 on v0

v1 whole, which is shorter than its diff:
```python
import jax
import jax.numpy as jnp
from jax import lax
from jax.experimental import pallas as pl
from jax.experimental.pallas import tpu as pltpu
from jax.sharding import PartitionSpec as P

F32, BF16 = jnp.float32, jnp.bfloat16
CHIPS = 8
MESH = pl.DeviceIdType.MESH


def chip_at(p):
    return p + lax.div(p, 4) * (11 - 2 * p)


def kernel(*refs):
    terms, weights, ms, vs = (refs[i : i + 3] for i in (0, 3, 6, 9))
    new_w, new_m, new_v, partner = (refs[i : i + 3] for i in (12, 15, 18, 21))
    wide, tall, own_wide, own_tall, w_wide, w_tall, m_wide, m_tall, v_wide, v_tall = refs[24:34]
    load_sem, state_sem, out_sem, d2d_send, d2d_recv, rs_send, rs_recv, ag_send, ag_recv, pair_send, pair_recv = refs[34:]

    me = lax.axis_index("dp")
    chip, core = lax.div(me, 2), lax.rem(me, 2)
    p = chip_at(chip)
    other = {"dp": 2 * chip + 1 - core}
    up = {"dp": 2 * chip_at(lax.rem(p + 1, CHIPS)) + core}
    down = {"dp": 2 * chip_at(lax.rem(p + CHIPS - 1, CHIPS)) + core}
    ahead = (up, down)

    barrier = pltpu.get_barrier_semaphore()
    for device in (up, down, other):
        pl.semaphore_signal(barrier, inc=1, device_id=device, device_id_type=MESH)
    pl.semaphore_wait(barrier, 3)

    def part(ref, index, way, which):
        if which == 2:
            return ref.at[(*index, way)]
        return ref.at[(*index, slice(None), pl.ds(2304 * way, 2304))]

    tasks = [(2 * which + layer, which, layer, way) for which in range(3) for layer in range(2) for way in range(2)]

    def block_of(way, back):
        return chip_at(lax.rem(p + CHIPS - back, CHIPS) if way == 0 else lax.rem(p + back, CHIPS))

    def sums(unit, which, way, k):
        return tall.at[unit - 4, way, k] if which == 2 else wide.at[unit, way, k]

    def to_partner(k, unit, which, layer, way):
        block = block_of(way, lax.rem(k + 1, CHIPS))
        return pltpu.make_async_remote_copy(
            part(terms[which], (layer, block, 1 - core), way, which),
            part(partner[which], (layer, block), way, which),
            d2d_send.at[unit, k, way],
            d2d_recv.at[unit, k, way],
            device_id=other,
            device_id_type=MESH,
        )

    def load(k, unit, which, layer, way):
        block = block_of(way, lax.rem(k + 1, CHIPS))
        mine = own_tall if which == 2 else own_wide
        return (
            pltpu.make_async_copy(part(terms[which], (layer, block, core), way, which), mine.at[way, 0], load_sem.at[way, 0]),
            pltpu.make_async_copy(part(partner[which], (layer, block), way, which), mine.at[way, 1], load_sem.at[way, 1]),
        )

    def start_load(k, task):
        to_partner(k, *task).wait_recv()
        for copy in load(k, *task):
            copy.start()

    def hop(k, unit, which, layer, way):
        return pltpu.make_async_remote_copy(
            sums(unit, which, way, k),
            sums(unit, which, way, k + 1),
            rs_send.at[unit, k, way],
            rs_recv.at[unit, k, way],
            device_id=ahead[way],
            device_id_type=MESH,
        )

    def state(unit, which, layer, way):
        w, m, v = (w_tall, m_tall, v_tall) if which == 2 else (w_wide, m_wide, v_wide)
        i = unit - 4 if which == 2 else unit
        return w.at[i, way], m.at[i, way], v.at[i, way]

    def load_state(unit, which, layer, way):
        w, m, v = state(unit, which, layer, way)
        return (
            pltpu.make_async_copy(part(weights[which], (layer, chip, core), way, which), w, state_sem.at[unit, way, 0]),
            pltpu.make_async_copy(part(ms[which], (layer,), way, which), m, state_sem.at[unit, way, 1]),
            pltpu.make_async_copy(part(vs[which], (layer,), way, which), v, state_sem.at[unit, way, 2]),
        )

    def store_state(unit, which, layer, way):
        _, m, v = state(unit, which, layer, way)
        return (
            pltpu.make_async_copy(sums(unit, which, way, 7), part(new_w[which], (layer, chip, core), way, which), out_sem.at[unit, way, 0]),
            pltpu.make_async_copy(m, part(new_m[which], (layer,), way, which), out_sem.at[unit, way, 1]),
            pltpu.make_async_copy(v, part(new_v[which], (layer,), way, which), out_sem.at[unit, way, 2]),
        )

    def forward(k, unit, which, layer, way, first):
        where = part(new_w[which], (layer, block_of(way, k), core), way, which)
        return pltpu.make_async_remote_copy(
            sums(unit, which, way, 7) if first else where,
            where,
            ag_send.at[unit, k, way],
            ag_recv.at[unit, k, way],
            device_id=ahead[way],
            device_id_type=MESH,
        )

    def arrival(k, unit, which, layer, way):
        where = part(new_w[which], (layer, block_of(way, k + 1), core), way, which)
        return pltpu.make_async_remote_copy(
            where, where, ag_send.at[unit, k, way], ag_recv.at[unit, k, way], device_id=ahead[way], device_id_type=MESH
        )

    def hand_over(k, unit, which, layer, way, first):
        where = part(new_w[which], (layer, block_of(way, k), core), way, which)
        return pltpu.make_async_remote_copy(
            sums(unit, which, way, 7) if first else where,
            where,
            pair_send.at[unit, k, way],
            pair_recv.at[unit, k, way],
            device_id=other,
            device_id_type=MESH,
        )

    def taken_over(k, unit, which, layer, way):
        where = part(new_w[which], (layer, block_of(way, k), 1 - core), way, which)
        return pltpu.make_async_remote_copy(
            where, where, pair_send.at[unit, k, way], pair_recv.at[unit, k, way], device_id=other, device_id_type=MESH
        )

    def columns(which):
        return 128 if which == 2 else 256

    def reduce_step(k, first):
        for i, task in enumerate(tasks):
            unit, which, layer, way = task
            if i + 1 < len(tasks):
                start_load(k, tasks[i + 1])
            for copy in load(k, *task):
                copy.wait()
            if not first:
                hop(k - 1, *task).wait_recv()
            total = sums(unit, which, way, k)
            mine = (own_tall if which == 2 else own_wide).at[way]
            size = columns(which)

            def add(j, _, total=total, mine=mine, size=size):
                at = (slice(None), pl.ds(pl.multiple_of(j * size, size), size))
                x = mine[(0, *at)].astype(F32) + mine[(1, *at)].astype(F32)
                if not first:
                    x = x + total[at].astype(F32)
                total[at] = x.astype(BF16)
                return 0

            lax.fori_loop(0, 9, add, 0)
            hop(k, *task).start()
            if i + 1 == len(tasks):
                start_load(k + 1, tasks[0])

    for k in range(2):
        for task in tasks:
            to_partner(k, *task).start()
    start_load(0, tasks[0])
    reduce_step(0, True)

    def reduce_loop(k, _):
        for task in tasks:
            to_partner(k + 1, *task).start()
        reduce_step(k, False)
        return 0

    for task in tasks:
        for copy in load_state(*task):
            copy.start()
    lax.fori_loop(1, 7, reduce_loop, 0)

    for i, task in enumerate(tasks):
        unit, which, layer, way = task
        if i + 1 < len(tasks):
            start_load(7, tasks[i + 1])
        for copy in load(7, *task) + load_state(*task):
            copy.wait()
        hop(6, *task).wait_recv()
        total = sums(unit, which, way, 7)
        mine = (own_tall if which == 2 else own_wide).at[way]
        w_ref, m_ref, v_ref = state(*task)
        size = columns(which)

        def adamw(j, _, total=total, mine=mine, w_ref=w_ref, m_ref=m_ref, v_ref=v_ref, size=size):
            at = (slice(None), pl.ds(pl.multiple_of(j * size, size), size))
            g = mine[(0, *at)].astype(F32) + mine[(1, *at)].astype(F32) + total[at].astype(F32)
            g = g.astype(BF16).astype(F32)
            w = w_ref[at].astype(F32)
            m = 0.9 * m_ref[at] + 0.1 * g
            v = 0.95 * v_ref[at] + 0.05 * g * g
            step = m * lax.rsqrt(v + 1e-8) + 0.1 * w
            total[at] = (w - 0.02 * step).astype(BF16)
            m_ref[at] = m
            v_ref[at] = v
            return 0

        lax.fori_loop(0, 9, adamw, 0)
        forward(0, *task, True).start()
        hand_over(0, *task, True).start()
        for copy in store_state(*task):
            copy.start()

    def gather_loop(k, _):
        for task in tasks:
            arrival(k - 1, *task).wait_recv()
            forward(k, *task, False).start()
            hand_over(k, *task, False).start()
        return 0

    lax.fori_loop(1, 7, gather_loop, 0)
    for task in tasks:
        arrival(6, *task).wait_recv()
        hand_over(7, *task, False).start()

    for task in tasks:
        for copy in store_state(*task):
            copy.wait()

    def drain(k, _):
        for task in tasks:
            hop(k, *task).wait_send()
            forward(k, *task, False).wait_send()
        return 0

    def drain_pair(k, _):
        for task in tasks:
            to_partner(k, *task).wait_send()
            hand_over(k, *task, False).wait_send()
            taken_over(k, *task).wait_recv()
        return 0

    lax.fori_loop(0, 7, drain, 0)
    lax.fori_loop(0, 8, drain_pair, 0)


def solution(mesh):
    def step(*arrays):
        terms = [arrays[0].reshape(2, 8, 2, 72, 4608), arrays[1].reshape(2, 8, 2, 72, 4608), arrays[2].reshape(2, 8, 2, 2, 144, 1152)]
        weights = [arrays[3].reshape(2, 8, 2, 72, 4608), arrays[4].reshape(2, 8, 2, 72, 4608), arrays[5].reshape(2, 8, 2, 2, 144, 1152)]
        moments = [a if i % 3 < 2 else a.reshape(2, 2, 144, 1152) for i, a in enumerate(arrays[6:])]
        wide_w = jax.ShapeDtypeStruct((2, 8, 2, 72, 4608), BF16)
        tall_w = jax.ShapeDtypeStruct((2, 8, 2, 2, 144, 1152), BF16)
        wide_m = jax.ShapeDtypeStruct((2, 72, 4608), F32)
        tall_m = jax.ShapeDtypeStruct((2, 2, 144, 1152), F32)
        wide_p = jax.ShapeDtypeStruct((2, 8, 72, 4608), BF16)
        tall_p = jax.ShapeDtypeStruct((2, 8, 2, 144, 1152), BF16)
        wide, tall = (72, 2304), (144, 1152)
        dma = pltpu.SemaphoreType.DMA
        out = pl.pallas_call(
            kernel,
            out_shape=(wide_w, wide_w, tall_w, *(wide_m, wide_m, tall_m) * 2, wide_p, wide_p, tall_p),
            in_specs=[pl.BlockSpec(memory_space=pl.ANY)] * 12,
            out_specs=[pl.BlockSpec(memory_space=pl.ANY)] * 12,
            scratch_shapes=[
                pltpu.VMEM((4, 2, 8, *wide), BF16),
                pltpu.VMEM((2, 2, 8, *tall), BF16),
                pltpu.VMEM((2, 2, *wide), BF16),
                pltpu.VMEM((2, 2, *tall), BF16),
                pltpu.VMEM((4, 2, *wide), BF16),
                pltpu.VMEM((2, 2, *tall), BF16),
                pltpu.VMEM((4, 2, *wide), F32),
                pltpu.VMEM((2, 2, *tall), F32),
                pltpu.VMEM((4, 2, *wide), F32),
                pltpu.VMEM((2, 2, *tall), F32),
                dma((2, 2)),
                dma((6, 2, 3)),
                dma((6, 2, 3)),
                dma((6, 8, 2)),
                dma((6, 8, 2)),
                dma((6, 7, 2)),
                dma((6, 7, 2)),
                dma((6, 7, 2)),
                dma((6, 7, 2)),
                dma((6, 8, 2)),
                dma((6, 8, 2)),
            ],
            compiler_params=pltpu.CompilerParams(collective_id=0, has_side_effects=True, vmem_limit_bytes=62 * 1024 * 1024),
        )(*terms, *weights, *moments)
        shapes = [a.shape for a in arrays[3:]]
        return tuple(a.reshape(s) for a, s in zip(out[:9], shapes, strict=True))

    all_of, cut = P(None, None, None), P(None, "dp", None)
    return jax.shard_map(
        step,
        mesh=mesh,
        in_specs=(P(("rep", "dp"), None, None, None),) * 3 + (all_of,) * 3 + (cut,) * 6,
        out_specs=(P("rep", None, None),) * 3 + (P("rep", "dp", None),) * 6,
        check_vma=False,
    )
```

time: 1040 us -> 674 us (0.65)
  waiting for transfers between devices: 732 us -> 0 us
  Pallas kernels: 0 us -> 614 us
  local copies, waits for them, and re-layouts: 272 us -> 57.9 us
  other arithmetic: 19.1 us -> 0.01 us
  between operations: 14.2 us -> 0.71 us
    pallas_call x0 -> x1, Pallas kernels: none -> 614 us  [step(): pl.pallas_call(kernel, out_shape=(wide_w, wide_w, tall_w, *(wide_m, wide_...]
    unnamed x8 -> x0, waiting for transfers between devices: 407 us -> none
    all_gather x3 -> x0, waiting for transfers between devices: 325 us -> none  [step(): whole = [lax.all_gather(one[0], 'dp', axis=1, tiled=True) for one in new]]
    unnamed x25 -> x35, local copies, waits for them, and re-layouts: 272 us -> 57.9 us
    convert_element_type x3 -> x0, other arithmetic: 19.1 us -> none  [adamw(): return ((w - 0.02 * step).astype(jnp.bfloat16), m, v)]
  transfers between devices with their start and end apart: 6 -> 0, of which waited for: 5 -> 0; matrix products, arithmetic and copies ran while one was open for 24% -> 0% of each run, Pallas kernels for 0% -> 0%
where the time goes in v1:
time: 674 us; the launch traced here: 673 us
  Pallas kernels  614 us (91%)
  local copies, waits for them, and re-layouts  57.9 us (9%)
    pallas_call x1, Pallas kernels, step(): pl.pallas_call(kernel, out_shape=(wide_w, wide_w, tall_w, *(wide_m, wide_...  614 us
    unnamed x35, local copies, waits for them, and re-layouts  57.9 us

profile of v1, /device:TPU:0, one launch (start us, length us, event | category | flops | bytes accessed | tf_op | source)
XLA Modules:
  0.0 672.8 jit_solution(16994321103947143741)
XLA Ops:
  0.6 614.1 %shard_map.187 = (bf16[2,8,2,72,4608]{4,3,2,1,0:T(8,128)(2,1)}, bf16[2,8,2,72,4608]{4,3,2,1,0:T(8,128)(2,1)}, bf16[2,8,2,2,144,1152]{5,4,3,2,1,0:T(8,128)(2,1)},...) custom-call(bf16[2,8,2,72,4608]{4,3,2,1,0:T(8,128)(2,1)} %bitcast.13, ...), custom_call_target="tpu_custom_call" | custom-call | tf_op jit(solution)/shard_map/pallas_call | solution.py:261
  614.8 0.0 copy-start
  614.8 0.0 slice-start
  614.8 0.0 slice-start.1
  614.8 0.0 slice-start.2
  614.8 21.0 %copy.30 = bf16[2,1152,4608]{2,1,0:T(8,128)(2,1)} copy(bf16[2,1152,4608]{2,1,0:T(8,128)(2,1)} %bitcast.23) | data formatting | bytes 42467328
  635.8 0.0 copy-done
  635.8 0.0 slice-start.3
  635.8 0.0 slice-start.5
  635.9 10.8 %copy.31 = bf16[2,1152,4608]{2,1,0:T(8,128)(2,1)} copy(bf16[2,1152,4608]{2,1,0:T(8,128)(2,1)S(1)} %bitcast.22) | data formatting | bytes 42467328
  646.6 0.0 slice-done
  646.6 0.0 slice-done.1
  646.6 0.0 slice-done.2
  646.6 2.0 slice-done.3
  648.6 1.2 slice-done.4
  649.8 0.0 slice-done.5
  649.8 0.0 copy-start.6
  649.8 8.0 %copy.32 = bf16[2,4608,1152]{2,1,0:T(8,128)(2,1)} copy(bf16[2,4608,1152]{2,1,0:T(8,128)(2,1)S(1)} %bitcast.21) | data formatting | bytes 42467328
  657.7 0.0 copy-done.6
  657.7 0.0 copy-start.5
  657.7 1.5 copy.33
  659.2 1.2 copy-done.5
  660.4 1.5 copy.34
  661.9 1.2 copy-done.4
  663.1 0.0 copy-start.3
  663.1 1.5 copy.35
  664.6 1.2 copy-done.3
  665.9 1.5 copy.36
  667.4 1.2 copy-done.2
  668.6 1.5 copy.37
  670.1 1.2 copy-done.1
  671.3 1.5 copy.38
  (5 shorter events, 0.0 us)
Async XLA Ops:
  614.8 21.0 %copy-start = (bf16[2,8,2,72,4608]{4,3,2,1,0:T(8,128)(2,1)S(1)}, bf16[2,8,2,72,4608]{4,3,2,1,0:T(8,128)(2,1)}, u32[]{:S(2)}) copy-start(bf16[2,8,2,72,4608]{4,3,2,1,0:T(8,128)(2,1)} %get-tuple-element.19) | copy-start | bytes 63700996
  614.8 31.8 %slice-start = ((s8[21233664]{0:T(1024)(128)(4,1)}), s8[4194304]{0:T(1024)(128)(4,1)S(1)}, s32[]{:S(2)}) async-start(s8[21233664]{0:T(1024)(128)(4,1)} %bitcast.19), calls=%async_computation | async-start | bytes 8388608
  614.8 31.8 %slice-start.1 = ((s8[21233664]{0:T(1024)(128)(4,1)}), s8[4194304]{0:T(1024)(128)(4,1)S(1)}, s32[]{:S(2)}) async-start(s8[21233664]{0:T(1024)(128)(4,1)} %bitcast.19), calls=%async_computation.1 | async-start | bytes 8388608
  614.8 31.8 %slice-start.2 = ((s8[21233664]{0:T(1024)(128)(4,1)}), s8[4194304]{0:T(1024)(128)(4,1)S(1)}, s32[]{:S(2)}) async-start(s8[21233664]{0:T(1024)(128)(4,1)} %bitcast.19), calls=%async_computation.2 | async-start | bytes 8388608
  635.8 12.7 %slice-start.3 = ((s8[21233664]{0:T(1024)(128)(4,1)}), s8[4194304]{0:T(1024)(128)(4,1)S(1)}, s32[]{:S(2)}) async-start(s8[21233664]{0:T(1024)(128)(4,1)} %bitcast.19), calls=%async_computation.3 | async-start | bytes 8388608
  635.8 13.9 %slice-start.4 = ((s8[21233664]{0:T(1024)(128)(4,1)}), s8[4194304]{0:T(1024)(128)(4,1)S(1)}, s32[]{:S(2)}) async-start(s8[21233664]{0:T(1024)(128)(4,1)} %bitcast.19), calls=%async_computation.4 | async-start | bytes 8388608
  635.8 13.9 %slice-start.5 = ((s8[21233664]{0:T(1024)(128)(4,1)}), s8[262144]{0:T(1024)(128)(4,1)S(1)}, s32[]{:S(2)}) async-start(s8[21233664]{0:T(1024)(128)(4,1)} %bitcast.19), calls=%async_computation.5 | async-start | bytes 524288
  649.8 8.0 %copy-start.6 = (f32[2,72,4608]{2,1,0:T(8,128)S(1)}, f32[2,72,4608]{2,1,0:T(8,128)}, u32[]{:S(2)}) copy-start(f32[2,72,4608]{2,1,0:T(8,128)} %get-tuple-element.39) | copy-start | bytes 7962628
  657.7 2.7 copy-start.5
  660.4 2.7 copy-start.4
  663.1 2.7 copy-start.3
  665.9 2.7 copy-start.2
  668.6 2.7 copy-start.1

commit v2 on v0

v2 whole, which is shorter than its diff:
```python
import jax
import jax.numpy as jnp
from jax import lax
from jax.experimental import pallas as pl
from jax.experimental.pallas import tpu as pltpu
from jax.sharding import PartitionSpec as P

F32, BF16 = jnp.float32, jnp.bfloat16
MESH = pl.DeviceIdType.MESH
UNITS = 24
ROWS, A, B, LANES = 72, 40, 32, 1152
LAG, B_STEP, B_OWN, B_OTHER, HAND, B_FIRST = 2, 4, 4, 5, 10, False


def lanes(body):
    def at(j, _):
        body(pl.ds(pl.multiple_of(j * 384, 384), 384))
        return 0

    lax.fori_loop(0, 3, at, 0)


def kernel(*refs):
    terms, weights, ms, vs = (refs[i : i + 3] for i in (0, 3, 6, 9))
    new_w, new_m, new_v = (refs[i : i + 3] for i in (12, 15, 18))
    partner, over_y = refs[21:23]
    xa, xb, out_y, out_z, in_z, la, lb, t_in, a_in, b_in, wa, wb, mv = refs[23:36]
    (
        pair_send, pair_recv, t_load, a_load, b_load, mv_load, wa_load, wb_load, sta, stb, own_a, own_b,
        y_send, y_recv, z_send, z_recv, xa_send, xa_recv, xb_send, xb_recv,
        ga_send, ga_recv, gb_send, gb_recv, ya_send, ya_recv, yb_send, yb_recv, hand_send, hand_recv,
    ) = refs[36:]

    me = lax.axis_index("dp")
    core = lax.rem(me, 2)
    z = lax.rem(lax.div(me, 2), 4)
    y = lax.div(me, 8)
    other = {"dp": me + 1 - 2 * core}
    across = {"dp": me + 8 - 16 * y}
    ahead = ({"dp": me + 2}, {"dp": me - 2})
    place = (z, 3 - z)

    barrier = pltpu.get_barrier_semaphore()
    for device in (other, across):
        pl.semaphore_signal(barrier, inc=1, device_id=device, device_id_type=MESH)
    for way in range(2):

        @pl.when(place[way] < 3)
        def _(way=way):
            pl.semaphore_signal(barrier, inc=1, device_id=ahead[way], device_id_type=MESH)

    pl.semaphore_wait(barrier, 2 + lax.div(z + 2, 3) + lax.div(5 - z, 3))

    def z_of(way, b):
        return b if way == 0 else 3 - b

    def each(u, body):
        for which in range(3):

            @pl.when(lax.div(u, 8) == which)
            def _(which=which):
                body(which, lax.rem(lax.div(u, 4), 2), lax.rem(u, 4))

    def cut(ref, which, lead, q, first, count):
        if which == 2:
            return ref.at[(*lead, q, pl.ds(first, count))]
        return ref.at[(*lead, pl.ds(first, count), pl.ds(pl.multiple_of(q * LANES, 128), LANES))]

    def send(source, target, sent, received, device):
        pltpu.make_async_remote_copy(source, target, sent, received, device_id=device, device_id_type=MESH).start()

    def arrived(like, sem, device=other):
        pltpu.make_async_remote_copy(like, like, sem, sem, device_id=device, device_id_type=MESH).wait_recv()

    def copied(like, sem):
        pltpu.make_async_copy(like, like, sem).wait()

    def to_partner(u):
        def go(which, layer, q):
            source = cut(terms[which], which, (layer, slice(None), slice(None), 1 - core), q, 0, ROWS)
            send(source, partner.at[u], pair_send.at[u], pair_recv.at[u], other)

        each(u, go)

    def load_t(u):
        arrived(partner.at[u], pair_recv.at[u])

        def go(which, layer, q):
            source = cut(terms[which], which, (layer, 1 - y, slice(None), core), q, 0, A)
            pltpu.make_async_copy(source, t_in.at[0], t_load.at[0]).start()

        each(u, go)
        pltpu.make_async_copy(partner.at[u, 1 - y, :, pl.ds(0, A)], t_in.at[1], t_load.at[1]).start()

    def sum_t(u, b):
        if b == 0:
            for i in range(2):
                copied(t_in.at[i], t_load.at[i])

        def body(c):
            out_y[u, b, :, c] = (t_in[0, b, :, c].astype(F32) + t_in[1, b, :, c].astype(F32)).astype(BF16)

        lanes(body)
        send(out_y.at[u, b], over_y.at[u, b], y_send.at[u], y_recv.at[u], across)

    def load_a(u):
        arrived(over_y.at[u], y_recv.at[u], across)

        def go(which, layer, q):
            source = cut(terms[which], which, (layer, y, slice(None), core), q, 0, A)
            pltpu.make_async_copy(source, a_in.at[0], a_load.at[0]).start()

        each(u, go)
        pltpu.make_async_copy(partner.at[u, y, :, pl.ds(0, A)], a_in.at[1], a_load.at[1]).start()
        pltpu.make_async_copy(over_y.at[u], a_in.at[2], a_load.at[2]).start()

    def sum_a(u, first, count):
        if first == 0:
            for i in range(3):
                copied(a_in.at[i], a_load.at[i])

        def one(b, _):
            def body(c):
                la[lax.rem(u, 3), b, :, c] = (
                    a_in[0, b, :, c].astype(F32) + a_in[1, b, :, c].astype(F32) + a_in[2, b, :, c].astype(F32)
                )

            lanes(body)
            return 0

        lax.fori_loop(first, first + count, one, 0)

    def load_b(u):
        def go(which, layer, q):
            source = cut(terms[which], which, (layer, slice(None), slice(None), core), q, A, B)
            pltpu.make_async_copy(source, b_in.at[0], b_load.at[0]).start()

        each(u, go)
        pltpu.make_async_copy(partner.at[u, :, :, pl.ds(A, B)], b_in.at[1], b_load.at[1]).start()

    def sum_b(u, first, count):
        if first == 0:
            for i in range(2):
                copied(b_in.at[i], b_load.at[i])

        def one(n, _):
            b, s = lax.div(n, 2), lax.rem(n, 2)

            def body(c):
                lb[lax.rem(u, 3), b, s, :, c] = b_in[0, s, b, :, c].astype(F32) + b_in[1, s, b, :, c].astype(F32)

            lanes(body)
            return 0

        lax.fori_loop(2 * first, 2 * (first + count), one, 0)

    def hop_a(u, way, b):
        i = place[way]
        x = xa.at[u, way, b - 1]
        mine = la.at[lax.rem(u, 3), z_of(way, b)]

        @pl.when(i == 0)
        def _():
            def body(c):
                x[:, c] = mine[:, c].astype(BF16)

            lanes(body)

        @pl.when(i > 0)
        def _():
            arrived(x, xa_recv.at[u, way, b - 1])

            def body(c):
                x[:, c] = (mine[:, c] + x[:, c].astype(F32)).astype(BF16)

            lanes(body)

        send(x, x, xa_send.at[u], xa_recv.at[u, way, b - 1], ahead[way])

    def hop_b(u, way, b):
        i = place[way]
        x = xb.at[u, way, b - 1]
        mine = lb.at[lax.rem(u, 3), z_of(way, b)]

        @pl.when(i == 0)
        def _():
            def body(c):
                for s in range(2):
                    x[s, :, c] = mine[s, :, c].astype(BF16)

            lanes(body)

        @pl.when(i > 0)
        def _():
            arrived(x, xb_recv.at[u, way, b - 1])

            def body(c):
                for s in range(2):
                    x[s, :, c] = (mine[s, :, c] + x[s, :, c].astype(F32)).astype(BF16)

            lanes(body)

        send(x, x, xb_send.at[u], xb_recv.at[u, way, b - 1], ahead[way])

    def load_state(u):
        @pl.when(u >= 3)
        def _():
            copied(mv.at[lax.rem(u, 3), :, pl.ds(0, A)], sta.at[lax.rem(u, 3)])
            copied(mv.at[lax.rem(u, 3), :, pl.ds(A, B)], stb.at[lax.rem(u, 3)])

        def go(which, layer, q):
            for i, from_ in enumerate((ms, vs)):
                source = cut(from_[which], which, (layer,), q, 0, ROWS)
                pltpu.make_async_copy(source, mv.at[lax.rem(u, 3), i], mv_load.at[lax.rem(u, 3)]).start()
            for buffer, sem, first, count in ((wa, wa_load, 0, A), (wb, wb_load, A, B)):
                source = cut(weights[which], which, (layer, y, z, core), q, first, count)
                pltpu.make_async_copy(source, buffer.at[u], sem.at[lax.rem(u, 3)]).start()

        each(u, go)

    def adamw(g, w_ref, u, first, count, c):
        rows = pl.ds(first, count)
        m_ref, v_ref = mv.at[lax.rem(u, 3), 0], mv.at[lax.rem(u, 3), 1]
        g = g.astype(BF16).astype(F32)
        w = w_ref[:, c].astype(F32)
        m = 0.9 * m_ref[rows, c] + 0.1 * g
        v = 0.95 * v_ref[rows, c] + 0.05 * g * g
        step = m * lax.rsqrt(v + 1e-8) + 0.1 * w
        w_ref[:, c] = (w - 0.02 * step).astype(BF16)
        m_ref[rows, c] = m
        v_ref[rows, c] = v

    def spread(which, layer, q, u, buffer, first, count, own_sem, st, across_sent, across_received, line_sent, line_received):
        where = cut(new_w[which], which, (layer, y, z, core), q, first, count)
        if line_sent is not None:
            for way in range(2):

                @pl.when(place[way] < 3)
                def _(way=way):
                    send(buffer.at[u], where, line_sent.at[u], line_received(way), ahead[way])

        send(buffer.at[u], where, across_sent.at[u], across_received.at[u], across)
        pltpu.make_async_copy(buffer.at[u], where, own_sem.at[u]).start()
        for i, to in enumerate((new_m, new_v)):
            target = cut(to[which], which, (layer,), q, first, count)
            pltpu.make_async_copy(mv.at[lax.rem(u, 3), i, pl.ds(first, count)], target, st.at[lax.rem(u, 3)]).start()

    def step_a(u):
        copied(wa.at[u], wa_load.at[lax.rem(u, 3)])
        mine = la.at[lax.rem(u, 3), z]
        for way in range(2):

            @pl.when(place[way] > 0)
            def _(way=way):
                x = xa.at[u, way, place[way] - 1]
                arrived(x, xa_recv.at[u, way, place[way] - 1])

                def body(c):
                    mine[:, c] = mine[:, c] + x[:, c].astype(F32)

                lanes(body)

        lanes(lambda c: adamw(mine[:, c], wa.at[u], u, 0, A, c))

        def go(which, layer, q):
            spread(which, layer, q, u, wa, 0, A, own_a, sta, ya_send, ya_recv, ga_send, lambda way: ga_recv.at[u, way, place[way]])

        each(u, go)

    def line_b(u):
        copied(mv.at[lax.rem(u, 3)], mv_load.at[lax.rem(u, 3)])
        mine = lb.at[lax.rem(u, 3), z]
        for way in range(2):

            @pl.when(place[way] > 0)
            def _(way=way):
                x = xb.at[u, way, place[way] - 1]
                arrived(x, xb_recv.at[u, way, place[way] - 1])

                def body(c):
                    for s in range(2):
                        mine[s, :, c] = mine[s, :, c] + x[s, :, c].astype(F32)

                lanes(body)

        def body(c):
            out_z[u, :, c] = mine[1 - y, :, c].astype(BF16)

        lanes(body)
        send(out_z.at[u], in_z.at[u], z_send.at[u], z_recv.at[u], across)

    def step_b(u):
        copied(wb.at[u], wb_load.at[lax.rem(u, 3)])
        arrived(in_z.at[u], z_recv.at[u], across)
        mine = lb.at[lax.rem(u, 3), z]
        lanes(lambda c: adamw(mine[y, :, c] + in_z[u, :, c].astype(F32), wb.at[u], u, A, B, c))

        def go(which, layer, q):
            spread(which, layer, q, u, wb, A, B, own_b, stb, yb_send, yb_recv, gb_send if B_OWN == B_STEP else None, lambda way: gb_recv.at[u, way, place[way], 0])

        each(u, go)

    def relay_a(u, way, b):
        arrived(wa.at[u], ga_recv.at[u, way, b])

        def go(which, layer, q):
            where = cut(new_w[which], which, (layer, y, z_of(way, b), core), q, 0, A)

            @pl.when(place[way] < 3)
            def _():
                send(where, where, ga_send.at[u], ga_recv.at[u, way, b], ahead[way])

            send(where, where, ya_send.at[u], ya_recv.at[u], across)

        each(u, go)

    def relay_b(u, way, b, s):
        arrived(wb.at[u], gb_recv.at[u, way, b, s])

        @pl.when(place[way] < 3)
        def _():
            def go(which, layer, q):
                row = y if s == 0 else 1 - y
                where = cut(new_w[which], which, (layer, row, z_of(way, b), core), q, A, B)
                send(where, where, gb_send.at[u], gb_recv.at[u, way, b, s], ahead[way])

            each(u, go)

    def own_b_out(u):
        def go(which, layer, q):
            where = cut(new_w[which], which, (layer, y, z, core), q, A, B)
            for way in range(2):

                @pl.when(place[way] < 3)
                def _(way=way):
                    send(wb.at[u], where, gb_send.at[u], gb_recv.at[u, way, place[way], 0], ahead[way])

        each(u, go)

    def from_across_b(u):
        arrived(wb.at[u], yb_recv.at[u], across)

        def go(which, layer, q):
            where = cut(new_w[which], which, (layer, 1 - y, z, core), q, A, B)
            for way in range(2):

                @pl.when(place[way] < 3)
                def _(way=way):
                    send(where, where, gb_send.at[u], gb_recv.at[u, way, place[way], 1], ahead[way])

        each(u, go)

    def hand_over(u):
        arrived(out_y.at[u], ya_recv.at[u], across)
        copied(wa.at[u], own_a.at[u])
        copied(wb.at[u], own_b.at[u])

        def go(which, layer, q):
            where = cut(new_w[which], which, (layer, slice(None), slice(None), core), q, 0, ROWS)
            send(where, where, hand_send.at[u], hand_recv.at[u], other)

        each(u, go)

    def when(condition, body, *args):
        @pl.when(condition)
        def _():
            body(*args)

    def hops_a(u, f):
        for way in range(2):
            when(place[way] <= f, hop_a, u, way, 3 - f + place[way])

    def hops_b(u, f):
        for way in range(2):
            when(place[way] <= f, hop_b, u, way, 3 - f + place[way])

    def relays_a(u, k):
        for way in range(2):
            when(place[way] >= k, relay_a, u, way, place[way] - k)

    def relays_b(u, k, s):
        for way in range(2):
            when(place[way] >= k, relay_b, u, way, place[way] - k, s)

    early = [(LAG + f, hops_a, f) for f in range(3)] + [(f, hops_b, f) for f in range(3)]
    early = early[::-1] if B_FIRST else early
    early += [(LAG + 3 + k, relays_a, k) for k in range(1, 4)]
    early += [(LAG + 3, step_a), (3, line_b)]
    middle = [(LAG - 8 + b, sum_t, b) for b in range(4)]
    middle += [(-4, sum_b, 0, 2), (-3, sum_b, 2, 2), (LAG - 2, sum_a, 0, 2), (LAG - 1, sum_a, 2, 2)]
    middle += [(-16, to_partner), (LAG - 9, load_t), (-7, load_b), (LAG - 3, load_a), (1, load_state)]
    late = [(B_OWN + k, relays_b, k, 0) for k in range(1, 4)] + [(B_OTHER + k, relays_b, k, 1) for k in range(1, 4)]
    late += [(B_STEP, step_b)] + ([(B_OWN, own_b_out)] if B_OWN != B_STEP else []) + [(B_OTHER, from_across_b), (HAND, hand_over)]

    to_partner(0)

    def period(r, _):
        for f in range(4):
            for offset, body, *rest in early + middle + late:
                if offset % 4 == f:
                    u = r - offset // 4
                    when(jnp.logical_and(u >= 0, u < UNITS), body, u, *rest)
        return 0

    lax.fori_loop(0, UNITS + 3 + HAND // 4, lambda n, _: period(n - 3, _), 0)

    for u in range(3):
        copied(mv.at[u, :, pl.ds(0, A)], sta.at[u])
        copied(mv.at[u, :, pl.ds(A, B)], stb.at[u])

    def sent(like, sem):
        pltpu.make_async_remote_copy(like, like, sem, sem, device_id=other, device_id_type=MESH).wait_send()

    inner = lax.div(z + 1, 2) == 1

    def drain(u, _):
        sent(partner.at[u], pair_send.at[u])
        sent(out_y.at[u], y_send.at[u])
        sent(out_z.at[u], z_send.at[u])
        sent(xa.at[u, 0], xa_send.at[u])
        sent(xb.at[u, 0], xb_send.at[u])
        sent(out_y.at[u], ya_send.at[u])
        sent(wb.at[u], yb_send.at[u])
        sent(partner.at[u], hand_send.at[u])

        @pl.when(inner)
        def _():
            sent(xa.at[pl.ds(0, 5), 0, 0], ga_send.at[u])
            sent(xb.at[pl.ds(0, 5), 0, 0], gb_send.at[u])

        @pl.when(jnp.logical_not(inner))
        def _():
            sent(xa.at[0, 0, 0], ga_send.at[u])
            sent(xb.at[0, 0, 0], gb_send.at[u])

        arrived(partner.at[u], hand_recv.at[u])
        return 0

    lax.fori_loop(0, UNITS, drain, 0)


def solution(mesh):
    def step(*arrays):
        def split(i, a):
            if i % 3 == 2:
                return a.reshape(2, 2, 4, 2, 4, ROWS, LANES)
            return a.reshape(2, 2, 4, 2, ROWS, 4 * LANES)

        whole = [split(i, a) for i, a in enumerate(arrays[:6])]
        moments = [a if i % 3 < 2 else a.reshape(2, 4, ROWS, LANES) for i, a in enumerate(arrays[6:])]
        dma = pltpu.SemaphoreType.DMA
        by_unit = dma((UNITS,))
        out = pl.pallas_call(
            kernel,
            out_shape=(
                *(jax.ShapeDtypeStruct(a.shape, a.dtype) for a in (*whole[3:], *moments)),
                jax.ShapeDtypeStruct((UNITS, 2, 4, ROWS, LANES), BF16),
                jax.ShapeDtypeStruct((UNITS, 4, A, LANES), BF16),
            ),
            in_specs=[pl.BlockSpec(memory_space=pl.ANY)] * 12,
            out_specs=[pl.BlockSpec(memory_space=pl.ANY)] * 11,
            scratch_shapes=[
                pltpu.VMEM((UNITS, 2, 3, A, LANES), BF16),
                pltpu.VMEM((UNITS, 2, 3, 2, B, LANES), BF16),
                pltpu.VMEM((UNITS, 4, A, LANES), BF16),
                pltpu.VMEM((UNITS, B, LANES), BF16),
                pltpu.VMEM((UNITS, B, LANES), BF16),
                pltpu.VMEM((3, 4, A, LANES), F32),
                pltpu.VMEM((3, 4, 2, B, LANES), F32),
                pltpu.VMEM((2, 4, A, LANES), BF16),
                pltpu.VMEM((3, 4, A, LANES), BF16),
                pltpu.VMEM((2, 2, 4, B, LANES), BF16),
                pltpu.VMEM((UNITS, A, LANES), BF16),
                pltpu.VMEM((UNITS, B, LANES), BF16),
                pltpu.VMEM((3, 2, ROWS, LANES), F32),
                *(by_unit, by_unit),
                *(dma((2,)), dma((3,)), dma((2,)), *(dma((3,)),) * 5, by_unit, by_unit),
                *(by_unit,) * 4,
                *(by_unit, dma((UNITS, 2, 3)), by_unit, dma((UNITS, 2, 3))),
                *(by_unit, dma((UNITS, 2, 3)), by_unit, dma((UNITS, 2, 3, 2))),
                *(by_unit,) * 6,
            ],
            compiler_params=pltpu.CompilerParams(collective_id=0, has_side_effects=True, vmem_limit_bytes=62 * 1024 * 1024),
        )(*whole, *moments)
        return tuple(a.reshape(like.shape) for a, like in zip(out[:9], arrays[3:], strict=True))

    all_of, cut = P(None, None, None), P(None, "dp", None)
    return jax.shard_map(
        step,
        mesh=mesh,
        in_specs=(P(("rep", "dp"), None, None, None),) * 3 + (all_of,) * 3 + (cut,) * 6,
        out_specs=(P("rep", None, None),) * 3 + (P("rep", "dp", None),) * 6,
        check_vma=False,
    )
```

time: 1040 us -> 609 us (0.59)
  waiting for transfers between devices: 732 us -> 0 us
  Pallas kernels: 0 us -> 550 us
  local copies, waits for them, and re-layouts: 272 us -> 57.9 us
  other arithmetic: 19.1 us -> 0.01 us
  between operations: 14.2 us -> 0.71 us
    pallas_call x0 -> x1, Pallas kernels: none -> 550 us  [step(): pl.pallas_call(kernel, out_shape=(*(jax.ShapeDtypeStruct(a.shape, a.dtype...]
    unnamed x8 -> x0, waiting for transfers between devices: 407 us -> none
    all_gather x3 -> x0, waiting for transfers between devices: 325 us -> none  [step(): whole = [lax.all_gather(one[0], 'dp', axis=1, tiled=True) for one in new]]
    unnamed x25 -> x35, local copies, waits for them, and re-layouts: 272 us -> 57.9 us
    convert_element_type x3 -> x0, other arithmetic: 19.1 us -> none  [adamw(): return ((w - 0.02 * step).astype(jnp.bfloat16), m, v)]
  transfers between devices with their start and end apart: 6 -> 0, of which waited for: 5 -> 0; matrix products, arithmetic and copies ran while one was open for 24% -> 0% of each run, Pallas kernels for 0% -> 0%
where the time goes in v2:
time: 609 us
  Pallas kernels  550 us (90%)
  local copies, waits for them, and re-layouts  57.9 us (10%)
    pallas_call x1, Pallas kernels, step(): pl.pallas_call(kernel, out_shape=(*(jax.ShapeDtypeStruct(a.shape, a.dtype...  550 us
    unnamed x35, local copies, waits for them, and re-layouts  57.9 us

profile of v2, /device:TPU:0, one launch (start us, length us, event | category | flops | bytes accessed | tf_op | source)
XLA Modules:
  0.0 608.8 jit_solution(4212572744764409052)
XLA Ops:
  0.6 550.1 %shard_map.187 = (bf16[2,2,4,2,72,4608]{5,4,3,2,1,0:T(8,128)(2,1)}, bf16[2,2,4,2,72,4608]{5,4,3,2,1,0:T(8,128)(2,1)}, bf16[2,2,4,2,4,72,1152]{6,5,4,3,2,1,0:T(8,...) custom-call(bf16[2,2,4,2,72,4608]{5,4,3,2,1,0:T(8,128)(2,1)} %bitcas, ...), custom_call_target="tpu_custom_call" | custom-call | tf_op jit(solution)/shard_map/pallas_call | solution.py:453
  550.8 0.0 copy-start
  550.8 0.0 slice-start
  550.8 0.0 slice-start.1
  550.8 0.0 slice-start.2
  550.8 21.0 %copy.30 = bf16[2,1152,4608]{2,1,0:T(8,128)(2,1)} copy(bf16[2,1152,4608]{2,1,0:T(8,128)(2,1)} %bitcast.23) | data formatting | bytes 42467328
  571.8 0.0 copy-done
  571.8 0.0 slice-start.3
  571.8 0.0 slice-start.4
  571.8 0.0 slice-start.5
  571.8 10.8 %copy.31 = bf16[2,1152,4608]{2,1,0:T(8,128)(2,1)} copy(bf16[2,1152,4608]{2,1,0:T(8,128)(2,1)S(1)} %bitcast.22) | data formatting | bytes 42467328
  582.6 0.0 slice-done
  582.6 0.0 slice-done.1
  582.6 0.0 slice-done.2
  582.6 2.0 slice-done.3
  584.5 1.2 slice-done.4
  585.7 0.0 slice-done.5
  585.7 0.0 copy-start.6
  585.7 8.0 %copy.32 = bf16[2,4608,1152]{2,1,0:T(8,128)(2,1)} copy(bf16[2,4608,1152]{2,1,0:T(8,128)(2,1)S(1)} %bitcast.21) | data formatting | bytes 42467328
  593.7 0.0 copy-done.6
  593.7 1.5 copy.33
  595.2 1.2 copy-done.5
  596.4 0.0 copy-start.4
  596.4 1.5 copy.34
  597.9 1.2 copy-done.4
  599.1 1.5 copy.35
  600.6 1.2 copy-done.3
  601.8 1.5 copy.36
  603.3 1.2 copy-done.2
  604.5 1.5 copy.37
  606.0 1.2 copy-done.1
  607.3 1.5 copy.38
  (5 shorter events, 0.0 us)
Async XLA Ops:
  550.8 21.0 %copy-start = (bf16[2,2,4,2,72,4608]{5,4,3,2,1,0:T(8,128)(2,1)S(1)}, bf16[2,2,4,2,72,4608]{5,4,3,2,1,0:T(8,128)(2,1)}, u32[]{:S(2)}) copy-start(bf16[2,2,4,2,72,4608]{5,4,3,2,1,0:T(8,128)(2,1)} %get-tuple-element.19) | copy-start | bytes 63700996
  550.8 31.8 %slice-start = ((s8[21233664]{0:T(1024)(128)(4,1)}), s8[4194304]{0:T(1024)(128)(4,1)S(1)}, s32[]{:S(2)}) async-start(s8[21233664]{0:T(1024)(128)(4,1)} %bitcast.19), calls=%async_computation | async-start | bytes 8388608
  550.8 31.8 %slice-start.1 = ((s8[21233664]{0:T(1024)(128)(4,1)}), s8[4194304]{0:T(1024)(128)(4,1)S(1)}, s32[]{:S(2)}) async-start(s8[21233664]{0:T(1024)(128)(4,1)} %bitcast.19), calls=%async_computation.1 | async-start | bytes 8388608
  550.8 31.8 %slice-start.2 = ((s8[21233664]{0:T(1024)(128)(4,1)}), s8[4194304]{0:T(1024)(128)(4,1)S(1)}, s32[]{:S(2)}) async-start(s8[21233664]{0:T(1024)(128)(4,1)} %bitcast.19), calls=%async_computation.2 | async-start | bytes 8388608
  571.8 12.7 %slice-start.3 = ((s8[21233664]{0:T(1024)(128)(4,1)}), s8[4194304]{0:T(1024)(128)(4,1)S(1)}, s32[]{:S(2)}) async-start(s8[21233664]{0:T(1024)(128)(4,1)} %bitcast.19), calls=%async_computation.3 | async-start | bytes 8388608
  571.8 13.9 %slice-start.4 = ((s8[21233664]{0:T(1024)(128)(4,1)}), s8[4194304]{0:T(1024)(128)(4,1)S(1)}, s32[]{:S(2)}) async-start(s8[21233664]{0:T(1024)(128)(4,1)} %bitcast.19), calls=%async_computation.4 | async-start | bytes 8388608
  571.8 13.9 %slice-start.5 = ((s8[21233664]{0:T(1024)(128)(4,1)}), s8[262144]{0:T(1024)(128)(4,1)S(1)}, s32[]{:S(2)}) async-start(s8[21233664]{0:T(1024)(128)(4,1)} %bitcast.19), calls=%async_computation.5 | async-start | bytes 524288
  585.7 8.0 %copy-start.6 = (f32[2,72,4608]{2,1,0:T(8,128)S(1)}, f32[2,72,4608]{2,1,0:T(8,128)}, u32[]{:S(2)}) copy-start(f32[2,72,4608]{2,1,0:T(8,128)} %get-tuple-element.39) | copy-start | bytes 7962628
  593.7 2.7 copy-start.5
  596.4 2.7 copy-start.4
  599.1 2.7 copy-start.3
  601.8 2.7 copy-start.2
  604.5 2.7 copy-start.1

commit v3 on v2

--- a/solution.py
+++ b/solution.py
@@ -8,6 +8,7 @@
 F32, BF16 = jnp.float32, jnp.bfloat16
 MESH = pl.DeviceIdType.MESH
 UNITS = 24
+RING, SLOTS = 4, 5
 ROWS, A, B, LANES = 72, 40, 32, 1152
 LAG, B_STEP, B_OWN, B_OTHER, HAND, B_FIRST = 2, 4, 4, 5, 10, False
 
@@ -22,14 +23,14 @@
 
 def kernel(*refs):
     terms, weights, ms, vs = (refs[i : i + 3] for i in (0, 3, 6, 9))
-    new_w, new_m, new_v = (refs[i : i + 3] for i in (12, 15, 18))
-    partner, over_y = refs[21:23]
-    xa, xb, out_y, out_z, in_z, la, lb, t_in, a_in, b_in, wa, wb, mv = refs[23:36]
+    new_w = refs[12:15]
+    mv, partner, over_y = refs[15:18]
+    xa, xb, out_y, out_z, in_z, la, lb, t_in, a_in, b_in, wa, wb = refs[18:30]
     (
-        pair_send, pair_recv, t_load, a_load, b_load, mv_load, wa_load, wb_load, sta, stb, own_a, own_b,
+        pair_send, pair_recv, t_load, a_load, b_load, mv_load, wa_load, wb_load, own_a, own_b,
         y_send, y_recv, z_send, z_recv, xa_send, xa_recv, xb_send, xb_recv,
         ga_send, ga_recv, gb_send, gb_recv, ya_send, ya_recv, yb_send, yb_recv, hand_send, hand_recv,
-    ) = refs[36:]
+    ) = refs[30:]
 
     me = lax.axis_index("dp")
     core = lax.rem(me, 2)
@@ -98,10 +99,10 @@
                 copied(t_in.at[i], t_load.at[i])
 
         def body(c):
-            out_y[u, b, :, c] = (t_in[0, b, :, c].astype(F32) + t_in[1, b, :, c].astype(F32)).astype(BF16)
+            out_y[lax.rem(u, RING), b, :, c] = (t_in[0, b, :, c].astype(F32) + t_in[1, b, :, c].astype(F32)).astype(BF16)
 
         lanes(body)
-        send(out_y.at[u, b], over_y.at[u, b], y_send.at[u], y_recv.at[u], across)
+        send(out_y.at[lax.rem(u, RING), b], over_y.at[u, b], y_send.at[u], y_recv.at[u], across)
 
     def load_a(u):
         arrived(over_y.at[u], y_recv.at[u], across)
@@ -156,7 +157,7 @@
 
     def hop_a(u, way, b):
         i = place[way]
-        x = xa.at[u, way, b - 1]
+        x = xa.at[lax.rem(u, RING), way, b - 1]
         mine = la.at[lax.rem(u, 3), z_of(way, b)]
 
         @pl.when(i == 0)
@@ -179,7 +180,7 @@
 
     def hop_b(u, way, b):
         i = place[way]
-        x = xb.at[u, way, b - 1]
+        x = xb.at[lax.rem(u, RING), way, b - 1]
         mine = lb.at[lax.rem(u, 3), z_of(way, b)]
 
         @pl.when(i == 0)
@@ -203,15 +204,10 @@
         send(x, x, xb_send.at[u], xb_recv.at[u, way, b - 1], ahead[way])
 
     def load_state(u):
-        @pl.when(u >= 3)
-        def _():
-            copied(mv.at[lax.rem(u, 3), :, pl.ds(0, A)], sta.at[lax.rem(u, 3)])
-            copied(mv.at[lax.rem(u, 3), :, pl.ds(A, B)], stb.at[lax.rem(u, 3)])
-
         def go(which, layer, q):
             for i, from_ in enumerate((ms, vs)):
                 source = cut(from_[which], which, (layer,), q, 0, ROWS)
-                pltpu.make_async_copy(source, mv.at[lax.rem(u, 3), i], mv_load.at[lax.rem(u, 3)]).start()
+                pltpu.make_async_copy(source, mv.at[u, i], mv_load.at[lax.rem(u, 3)]).start()
             for buffer, sem, first, count in ((wa, wa_load, 0, A), (wb, wb_load, A, B)):
                 source = cut(weights[which], which, (layer, y, z, core), q, first, count)
                 pltpu.make_async_copy(source, buffer.at[u], sem.at[lax.rem(u, 3)]).start()
@@ -220,7 +216,7 @@
 
     def adamw(g, w_ref, u, first, count, c):
         rows = pl.ds(first, count)
-        m_ref, v_ref = mv.at[lax.rem(u, 3), 0], mv.at[lax.rem(u, 3), 1]
+        m_ref, v_ref = mv.at[u, 0], mv.at[u, 1]
         g = g.astype(BF16).astype(F32)
         w = w_ref[:, c].astype(F32)
         m = 0.9 * m_ref[rows, c] + 0.1 * g
@@ -230,7 +226,7 @@
         m_ref[rows, c] = m
         v_ref[rows, c] = v
 
-    def spread(which, layer, q, u, buffer, first, count, own_sem, st, across_sent, across_received, line_sent, line_received):
+    def spread(which, layer, q, u, buffer, first, count, own_sem, across_sent, across_received, line_sent, line_received):
         where = cut(new_w[which], which, (layer, y, z, core), q, first, count)
         if line_sent is not None:
             for way in range(2):
@@ -241,9 +237,6 @@
 
         send(buffer.at[u], where, across_sent.at[u], across_received.at[u], across)
         pltpu.make_async_copy(buffer.at[u], where, own_sem.at[u]).start()
-        for i, to in enumerate((new_m, new_v)):
-            target = cut(to[which], which, (layer,), q, first, count)
-            pltpu.make_async_copy(mv.at[lax.rem(u, 3), i, pl.ds(first, count)], target, st.at[lax.rem(u, 3)]).start()
 
     def step_a(u):
         copied(wa.at[u], wa_load.at[lax.rem(u, 3)])
@@ -252,7 +245,7 @@
 
             @pl.when(place[way] > 0)
             def _(way=way):
-                x = xa.at[u, way, place[way] - 1]
+                x = xa.at[lax.rem(u, RING), way, place[way] - 1]
                 arrived(x, xa_recv.at[u, way, place[way] - 1])
 
                 def body(c):
@@ -263,18 +256,18 @@
         lanes(lambda c: adamw(mine[:, c], wa.at[u], u, 0, A, c))
 
         def go(which, layer, q):
-            spread(which, layer, q, u, wa, 0, A, own_a, sta, ya_send, ya_recv, ga_send, lambda way: ga_recv.at[u, way, place[way]])
+            spread(which, layer, q, u, wa, 0, A, own_a, ya_send, ya_recv, ga_send, lambda way: ga_recv.at[u, way, place[way]])
 
         each(u, go)
 
     def line_b(u):
-        copied(mv.at[lax.rem(u, 3)], mv_load.at[lax.rem(u, 3)])
+        copied(mv.at[u], mv_load.at[lax.rem(u, 3)])
         mine = lb.at[lax.rem(u, 3), z]
         for way in range(2):
 
             @pl.when(place[way] > 0)
             def _(way=way):
-                x = xb.at[u, way, place[way] - 1]
+                x = xb.at[lax.rem(u, RING), way, place[way] - 1]
                 arrived(x, xb_recv.at[u, way, place[way] - 1])
 
                 def body(c):
@@ -296,7 +289,7 @@
         lanes(lambda c: adamw(mine[y, :, c] + in_z[u, :, c].astype(F32), wb.at[u], u, A, B, c))
 
         def go(which, layer, q):
-            spread(which, layer, q, u, wb, A, B, own_b, stb, yb_send, yb_recv, gb_send if B_OWN == B_STEP else None, lambda way: gb_recv.at[u, way, place[way], 0])
+            spread(which, layer, q, u, wb, A, B, own_b, yb_send, yb_recv, gb_send if B_OWN == B_STEP else None, lambda way: gb_recv.at[u, way, place[way], 0])
 
         each(u, go)
 
@@ -351,7 +344,7 @@
         each(u, go)
 
     def hand_over(u):
-        arrived(out_y.at[u], ya_recv.at[u], across)
+        arrived(out_y.at[0], ya_recv.at[u], across)
         copied(wa.at[u], own_a.at[u])
         copied(wb.at[u], own_b.at[u])
 
@@ -381,14 +374,24 @@
     def relays_b(u, k, s):
         for way in range(2):
             when(place[way] >= k, relay_b, u, way, place[way] - k, s)
+
+    def sent(like, sem):
+        pltpu.make_async_remote_copy(like, like, sem, sem, device_id=other, device_id_type=MESH).wait_send()
+
+    def free_x(u):
+        sent(xa.at[0, 0], xa_send.at[u])
+        sent(xb.at[0, 0], xb_send.at[u])
+
+    def free_y(u):
+        sent(out_y.at[0], y_send.at[u])
 
     early = [(LAG + f, hops_a, f) for f in range(3)] + [(f, hops_b, f) for f in range(3)]
     early = early[::-1] if B_FIRST else early
     early += [(LAG + 3 + k, relays_a, k) for k in range(1, 4)]
     early += [(LAG + 3, step_a), (3, line_b)]
     middle = [(LAG - 8 + b, sum_t, b) for b in range(4)]
-    middle += [(-4, sum_b, 0, 2), (-3, sum_b, 2, 2), (LAG - 2, sum_a, 0, 2), (LAG - 1, sum_a, 2, 2)]
-    middle += [(-16, to_partner), (LAG - 9, load_t), (-7, load_b), (LAG - 3, load_a), (1, load_state)]
+    middle += [(-4, sum_b, 0, 2), (-3, sum_b, 2, 2), (LAG - 1, sum_a, 0, 4)]
+    middle += [(-16, to_partner), (LAG - 9, load_t), (-7, load_b), (LAG - 2, load_a), (1, load_state), (8, free_x), (3, free_y)]
     late = [(B_OWN + k, relays_b, k, 0) for k in range(1, 4)] + [(B_OTHER + k, relays_b, k, 1) for k in range(1, 4)]
     late += [(B_STEP, step_b)] + ([(B_OWN, own_b_out)] if B_OWN != B_STEP else []) + [(B_OTHER, from_across_b), (HAND, hand_over)]
 
@@ -404,39 +407,64 @@
 
     lax.fori_loop(0, UNITS + 3 + HAND // 4, lambda n, _: period(n - 3, _), 0)
 
-    for u in range(3):
-        copied(mv.at[u, :, pl.ds(0, A)], sta.at[u])
-        copied(mv.at[u, :, pl.ds(A, B)], stb.at[u])
-
-    def sent(like, sem):
-        pltpu.make_async_remote_copy(like, like, sem, sem, device_id=other, device_id_type=MESH).wait_send()
-
     inner = lax.div(z + 1, 2) == 1
 
     def drain(u, _):
         sent(partner.at[u], pair_send.at[u])
-        sent(out_y.at[u], y_send.at[u])
         sent(out_z.at[u], z_send.at[u])
-        sent(xa.at[u, 0], xa_send.at[u])
-        sent(xb.at[u, 0], xb_send.at[u])
-        sent(out_y.at[u], ya_send.at[u])
+        sent(out_y.at[0], ya_send.at[u])
         sent(wb.at[u], yb_send.at[u])
         sent(partner.at[u], hand_send.at[u])
 
         @pl.when(inner)
         def _():
-            sent(xa.at[pl.ds(0, 5), 0, 0], ga_send.at[u])
-            sent(xb.at[pl.ds(0, 5), 0, 0], gb_send.at[u])
+            sent(wa.at[pl.ds(0, 5)], ga_send.at[u])
+            sent(wb.at[pl.ds(0, 10)], gb_send.at[u])
 
         @pl.when(jnp.logical_not(inner))
         def _():
-            sent(xa.at[0, 0, 0], ga_send.at[u])
-            sent(xb.at[0, 0, 0], gb_send.at[u])
+            sent(wa.at[0], ga_send.at[u])
+            sent(wb.at[pl.ds(0, 2)], gb_send.at[u])
 
         arrived(partner.at[u], hand_recv.at[u])
         return 0
 
     lax.fori_loop(0, UNITS, drain, 0)
+
+
+def unload(gate, up, down, mv, *refs):
+    new_w, new_m, new_v = refs[:3], refs[3:6], refs[6:9]
+    slots, in_sem, out_sem, down_sem, mv_sem = refs[9:]
+    chunks = [(which, layer, row, half) for which in range(2) for layer in range(2) for row in range(2) for half in range(2)]
+    sources = (gate, up, down)
+
+    def read(n):
+        which, layer, row, half = chunks[n]
+        return pltpu.make_async_copy(sources[which].at[layer, row, pl.ds(2 * half, 2)], slots.at[n % SLOTS], in_sem.at[n % SLOTS])
+
+    def write(n):
+        which, layer, row, half = chunks[n]
+        return pltpu.make_async_copy(slots.at[n % SLOTS], new_w[which].at[layer, row, pl.ds(2 * half, 2)], out_sem.at[n % SLOTS])
+
+    for n in range(SLOTS):
+        read(n).start()
+    pltpu.make_async_copy(down, new_w[2], down_sem).start()
+    for u in range(UNITS):
+        which, layer, q = u // 8, u // 4 % 2, u % 4
+        for i, to in enumerate((new_m, new_v)):
+            target = to[which].at[layer, q] if which == 2 else to[which].at[layer, :, pl.ds(q * LANES, LANES)]
+            pltpu.make_async_copy(mv.at[u, i], target, mv_sem).start()
+    for n in range(len(chunks)):
+        read(n).wait()
+        write(n).start()
+        ahead = n + SLOTS - 2
+        if n >= 2 and ahead < len(chunks):
+            write(ahead - SLOTS).wait()
+            read(ahead).start()
+    for n in range(len(chunks) - SLOTS, len(chunks)):
+        write(n).wait()
+    pltpu.make_async_copy(down, down, down_sem).wait()
+    pltpu.make_async_copy(mv, mv, mv_sem).wait()
 
 
 def solution(mesh):
@@ -450,19 +478,22 @@
         moments = [a if i % 3 < 2 else a.reshape(2, 4, ROWS, LANES) for i, a in enumerate(arrays[6:])]
         dma = pltpu.SemaphoreType.DMA
         by_unit = dma((UNITS,))
+        hbm = [jax.ShapeDtypeStruct(a.shape, a.dtype) for a in whole[3:]]
+        kept = [pltpu.VMEM(whole[5].shape, BF16), pltpu.VMEM((UNITS, 2, ROWS, LANES), F32)]
         out = pl.pallas_call(
             kernel,
             out_shape=(
-                *(jax.ShapeDtypeStruct(a.shape, a.dtype) for a in (*whole[3:], *moments)),
+                *hbm[:2],
+                *kept,
                 jax.ShapeDtypeStruct((UNITS, 2, 4, ROWS, LANES), BF16),
                 jax.ShapeDtypeStruct((UNITS, 4, A, LANES), BF16),
             ),
             in_specs=[pl.BlockSpec(memory_space=pl.ANY)] * 12,
-            out_specs=[pl.BlockSpec(memory_space=pl.ANY)] * 11,
+            out_specs=[pl.BlockSpec(memory_space=space) for space in (pl.ANY, pl.ANY, pltpu.VMEM, pltpu.VMEM, pl.ANY, pl.ANY)],
             scratch_shapes=[
-                pltpu.VMEM((UNITS, 2, 3, A, LANES), BF16),
-                pltpu.VMEM((UNITS, 2, 3, 2, B, LANES), BF16),
-                pltpu.VMEM((UNITS, 4, A, LANES), BF16),
+                pltpu.VMEM((RING, 2, 3, A, LANES), BF16),
+                pltpu.VMEM((RING, 2, 3, 2, B, LANES), BF16),
+                pltpu.VMEM((RING, 4, A, LANES), BF16),
                 pltpu.VMEM((UNITS, B, LANES), BF16),
                 pltpu.VMEM((UNITS, B, LANES), BF16),
                 pltpu.VMEM((3, 4, A, LANES), F32),
@@ -472,17 +503,24 @@
                 pltpu.VMEM((2, 2, 4, B, LANES), BF16),
                 pltpu.VMEM((UNITS, A, LANES), BF16),
                 pltpu.VMEM((UNITS, B, LANES), BF16),
-                pltpu.VMEM((3, 2, ROWS, LANES), F32),
                 *(by_unit, by_unit),
-                *(dma((2,)), dma((3,)), dma((2,)), *(dma((3,)),) * 5, by_unit, by_unit),
+                *(dma((2,)), dma((3,)), dma((2,)), *(dma((3,)),) * 3, by_unit, by_unit),
                 *(by_unit,) * 4,
                 *(by_unit, dma((UNITS, 2, 3)), by_unit, dma((UNITS, 2, 3))),
                 *(by_unit, dma((UNITS, 2, 3)), by_unit, dma((UNITS, 2, 3, 2))),
                 *(by_unit,) * 6,
             ],
-            compiler_params=pltpu.CompilerParams(collective_id=0, has_side_effects=True, vmem_limit_bytes=62 * 1024 * 1024),
+            compiler_params=pltpu.CompilerParams(collective_id=0, has_side_effects=True, vmem_limit_bytes=24 * 1024 * 1024),
         )(*whole, *moments)
-        return tuple(a.reshape(like.shape) for a, like in zip(out[:9], arrays[3:], strict=True))
+        final = pl.pallas_call(
+            unload,
+            out_shape=(*hbm, *(jax.ShapeDtypeStruct(a.shape, a.dtype) for a in moments)),
+            in_specs=[pl.BlockSpec(memory_space=space) for space in (pltpu.HBM, pltpu.HBM, pltpu.VMEM, pltpu.VMEM)],
+            out_specs=[pl.BlockSpec(memory_space=pl.ANY)] * 9,
+            scratch_shapes=[pltpu.VMEM((SLOTS, 2, 2, ROWS, 4 * LANES), BF16), dma((SLOTS,)), dma((SLOTS,)), dma, dma],
+            compiler_params=pltpu.CompilerParams(vmem_limit_bytes=24 * 1024 * 1024),
+        )(*(pltpu.with_memory_space_constraint(a, space) for a, space in zip(out[:4], (pltpu.HBM, pltpu.HBM, pltpu.VMEM, pltpu.VMEM), strict=True)))
+        return tuple(a.reshape(like.shape) for a, like in zip(final, arrays[3:], strict=True))
 
     all_of, cut = P(None, None, None), P(None, "dp", None)
     return jax.shard_map(

time: 609 us -> 591 us (0.970)
  local copies, waits for them, and re-layouts: 57.9 us -> 0 us
  Pallas kernels: 550 us -> 590 us
    unnamed x35 -> x0, local copies, waits for them, and re-layouts: 57.9 us -> none
    pallas_call x1 -> x2, Pallas kernels: 550 us -> 590 us  [the longest x1 550 us: step(): pl.pallas_call(kernel, out_shape=(*hbm[:2], *kept, jax.ShapeDtypeStruct((...]
where the time goes in v3:
time: 591 us
  Pallas kernels  590 us (100%)
    pallas_call x1, Pallas kernels, step(): pl.pallas_call(kernel, out_shape=(*hbm[:2], *kept, jax.ShapeDtypeStruct((...  550 us
    pallas_call x1, Pallas kernels, step(): pl.pallas_call(unload, out_shape=(*hbm, *(jax.ShapeDtypeStruct(a.shape, a...  39.5 us

profile of v3, /device:TPU:0, one launch (start us, length us, event | category | flops | bytes accessed | tf_op | source)
XLA Modules:
  0.0 590.5 jit_solution(12480389278121041069)
XLA Ops:
  0.6 550.3 %shard_map.187 = (bf16[2,2,4,2,72,4608]{5,4,3,2,1,0:T(8,128)(2,1)}, bf16[2,2,4,2,72,4608]{5,4,3,2,1,0:T(8,128)(2,1)}, bf16[2,2,4,2,4,72,1152]{6,5,4,3,2,1,0:T(8,...) custom-call(bf16[2,2,4,2,72,4608]{5,4,3,2,1,0:T(8,128)(2,1)} %bitcas, ...), custom_call_target="tpu_custom_call" | custom-call | tf_op jit(solution)/shard_map/pallas_call | solution.py:483
  551.0 39.5 %shard_map.188 = (bf16[2,2,4,2,72,4608]{5,4,3,2,1,0:T(8,128)(2,1)}, bf16[2,2,4,2,72,4608]{5,4,3,2,1,0:T(8,128)(2,1)}, bf16[2,2,4,2,4,72,1152]{6,5,4,3,2,1,0:T(8,...) custom-call(bf16[2,2,4,2,72,4608]{5,4,3,2,1,0:T(8,128)(2,1)} %get-tu, ...), custom_call_target="tpu_custom_call" | custom-call | tf_op jit(solution)/shard_map/pallas_call | solution.py:515

commit v4 on v3

--- a/solution.py
+++ b/solution.py
@@ -10,6 +10,7 @@
 UNITS = 24
 RING, SLOTS = 4, 5
 ROWS, A, B, LANES = 72, 40, 32, 1152
+GA, GB = 48, 24
 LAG, B_STEP, B_OWN, B_OTHER, HAND, B_FIRST = 2, 4, 4, 5, 10, False
 
 
@@ -25,12 +26,12 @@
     terms, weights, ms, vs = (refs[i : i + 3] for i in (0, 3, 6, 9))
     new_w = refs[12:15]
     mv, partner, over_y = refs[15:18]
-    xa, xb, out_y, out_z, in_z, la, lb, t_in, a_in, b_in, wa, wb = refs[18:30]
+    xa, xb, out_y, out_z, in_z, la, lb, t_in, a_in, b_in, w_own = refs[18:29]
     (
-        pair_send, pair_recv, t_load, a_load, b_load, mv_load, wa_load, wb_load, own_a, own_b,
+        pair_send, pair_recv, t_load, a_load, b_load, mv_load, w_load, own_a, own_b,
         y_send, y_recv, z_send, z_recv, xa_send, xa_recv, xb_send, xb_recv,
         ga_send, ga_recv, gb_send, gb_recv, ya_send, ya_recv, yb_send, yb_recv, hand_send, hand_recv,
-    ) = refs[30:]
+    ) = refs[29:]
 
     me = lax.axis_index("dp")
     core = lax.rem(me, 2)
@@ -208,38 +209,37 @@
             for i, from_ in enumerate((ms, vs)):
                 source = cut(from_[which], which, (layer,), q, 0, ROWS)
                 pltpu.make_async_copy(source, mv.at[u, i], mv_load.at[lax.rem(u, 3)]).start()
-            for buffer, sem, first, count in ((wa, wa_load, 0, A), (wb, wb_load, A, B)):
-                source = cut(weights[which], which, (layer, y, z, core), q, first, count)
-                pltpu.make_async_copy(source, buffer.at[u], sem.at[lax.rem(u, 3)]).start()
-
-        each(u, go)
-
-    def adamw(g, w_ref, u, first, count, c):
+            source = cut(weights[which], which, (layer, y, z, core), q, 0, ROWS)
+            pltpu.make_async_copy(source, w_own.at[u], w_load.at[lax.rem(u, 3)]).start()
+
+        each(u, go)
+
+    def adamw(g, u, first, count, c):
         rows = pl.ds(first, count)
-        m_ref, v_ref = mv.at[u, 0], mv.at[u, 1]
+        w_ref, m_ref, v_ref = w_own.at[u], mv.at[u, 0], mv.at[u, 1]
         g = g.astype(BF16).astype(F32)
-        w = w_ref[:, c].astype(F32)
+        w = w_ref[rows, c].astype(F32)
         m = 0.9 * m_ref[rows, c] + 0.1 * g
         v = 0.95 * v_ref[rows, c] + 0.05 * g * g
         step = m * lax.rsqrt(v + 1e-8) + 0.1 * w
-        w_ref[:, c] = (w - 0.02 * step).astype(BF16)
+        w_ref[rows, c] = (w - 0.02 * step).astype(BF16)
         m_ref[rows, c] = m
         v_ref[rows, c] = v
 
-    def spread(which, layer, q, u, buffer, first, count, own_sem, across_sent, across_received, line_sent, line_received):
+    def spread(which, layer, q, u, first, count, own_sem, across_sent, across_received, line_sent, line_received):
         where = cut(new_w[which], which, (layer, y, z, core), q, first, count)
+        source = w_own.at[u, pl.ds(first, count)]
         if line_sent is not None:
             for way in range(2):
 
                 @pl.when(place[way] < 3)
                 def _(way=way):
-                    send(buffer.at[u], where, line_sent.at[u], line_received(way), ahead[way])
-
-        send(buffer.at[u], where, across_sent.at[u], across_received.at[u], across)
-        pltpu.make_async_copy(buffer.at[u], where, own_sem.at[u]).start()
+                    send(source, where, line_sent.at[u], line_received(way), ahead[way])
+
+        send(source, where, across_sent.at[u], across_received.at[u], across)
+        pltpu.make_async_copy(source, where, own_sem.at[u]).start()
 
     def step_a(u):
-        copied(wa.at[u], wa_load.at[lax.rem(u, 3)])
         mine = la.at[lax.rem(u, 3), z]
         for way in range(2):
 
@@ -253,15 +253,16 @@
 
                 lanes(body)
 
-        lanes(lambda c: adamw(mine[:, c], wa.at[u], u, 0, A, c))
-
-        def go(which, layer, q):
-            spread(which, layer, q, u, wa, 0, A, own_a, ya_send, ya_recv, ga_send, lambda way: ga_recv.at[u, way, place[way]])
+        lanes(lambda c: adamw(mine[:, c], u, 0, A, c))
+
+        def go(which, layer, q):
+            spread(which, layer, q, u, 0, GA, own_a, ya_send, ya_recv, ga_send, lambda way: ga_recv.at[u, way, place[way]])
 
         each(u, go)
 
     def line_b(u):
         copied(mv.at[u], mv_load.at[lax.rem(u, 3)])
+        copied(w_own.at[u], w_load.at[lax.rem(u, 3)])
         mine = lb.at[lax.rem(u, 3), z]
         for way in range(2):
 
@@ -283,21 +284,20 @@
         send(out_z.at[u], in_z.at[u], z_send.at[u], z_recv.at[u], across)
 
     def step_b(u):
-        copied(wb.at[u], wb_load.at[lax.rem(u, 3)])
         arrived(in_z.at[u], z_recv.at[u], across)
         mine = lb.at[lax.rem(u, 3), z]
-        lanes(lambda c: adamw(mine[y, :, c] + in_z[u, :, c].astype(F32), wb.at[u], u, A, B, c))
-
-        def go(which, layer, q):
-            spread(which, layer, q, u, wb, A, B, own_b, yb_send, yb_recv, gb_send if B_OWN == B_STEP else None, lambda way: gb_recv.at[u, way, place[way], 0])
+        lanes(lambda c: adamw(mine[y, :, c] + in_z[u, :, c].astype(F32), u, A, B, c))
+
+        def go(which, layer, q):
+            spread(which, layer, q, u, GA, GB, own_b, yb_send, yb_recv, gb_send if B_OWN == B_STEP else None, lambda way: gb_recv.at[u, way, place[way], 0])
 
         each(u, go)
 
     def relay_a(u, way, b):
-        arrived(wa.at[u], ga_recv.at[u, way, b])
-
-        def go(which, layer, q):
-            where = cut(new_w[which], which, (layer, y, z_of(way, b), core), q, 0, A)
+        arrived(w_own.at[u, pl.ds(0, GA)], ga_recv.at[u, way, b])
+
+        def go(which, layer, q):
+            where = cut(new_w[which], which, (layer, y, z_of(way, b), core), q, 0, GA)
 
             @pl.when(place[way] < 3)
             def _():
@@ -308,33 +308,33 @@
         each(u, go)
 
     def relay_b(u, way, b, s):
-        arrived(wb.at[u], gb_recv.at[u, way, b, s])
+        arrived(w_own.at[u, pl.ds(GA, GB)], gb_recv.at[u, way, b, s])
 
         @pl.when(place[way] < 3)
         def _():
             def go(which, layer, q):
                 row = y if s == 0 else 1 - y
-                where = cut(new_w[which], which, (layer, row, z_of(way, b), core), q, A, B)
+                where = cut(new_w[which], which, (layer, row, z_of(way, b), core), q, GA, GB)
                 send(where, where, gb_send.at[u], gb_recv.at[u, way, b, s], ahead[way])
 
             each(u, go)
 
     def own_b_out(u):
         def go(which, layer, q):
-            where = cut(new_w[which], which, (layer, y, z, core), q, A, B)
+            where = cut(new_w[which], which, (layer, y, z, core), q, GA, GB)
             for way in range(2):
 
                 @pl.when(place[way] < 3)
                 def _(way=way):
-                    send(wb.at[u], where, gb_send.at[u], gb_recv.at[u, way, place[way], 0], ahead[way])
+                    send(w_own.at[u, pl.ds(GA, GB)], where, gb_send.at[u], gb_recv.at[u, way, place[way], 0], ahead[way])
 
         each(u, go)
 
     def from_across_b(u):
-        arrived(wb.at[u], yb_recv.at[u], across)
-
-        def go(which, layer, q):
-            where = cut(new_w[which], which, (layer, 1 - y, z, core), q, A, B)
+        arrived(w_own.at[u, pl.ds(GA, GB)], yb_recv.at[u], across)
+
+        def go(which, layer, q):
+            where = cut(new_w[which], which, (layer, 1 - y, z, core), q, GA, GB)
             for way in range(2):
 
                 @pl.when(place[way] < 3)
@@ -344,9 +344,9 @@
         each(u, go)
 
     def hand_over(u):
-        arrived(out_y.at[0], ya_recv.at[u], across)
-        copied(wa.at[u], own_a.at[u])
-        copied(wb.at[u], own_b.at[u])
+        arrived(w_own.at[pl.ds(0, 4), pl.ds(0, GA)], ya_recv.at[u], across)
+        copied(w_own.at[u, pl.ds(0, GA)], own_a.at[u])
+        copied(w_own.at[u, pl.ds(GA, GB)], own_b.at[u])
 
         def go(which, layer, q):
             where = cut(new_w[which], which, (layer, slice(None), slice(None), core), q, 0, ROWS)
@@ -412,19 +412,19 @@
     def drain(u, _):
         sent(partner.at[u], pair_send.at[u])
         sent(out_z.at[u], z_send.at[u])
-        sent(out_y.at[0], ya_send.at[u])
-        sent(wb.at[u], yb_send.at[u])
+        sent(w_own.at[pl.ds(0, 4), pl.ds(0, GA)], ya_send.at[u])
+        sent(w_own.at[u, pl.ds(GA, GB)], yb_send.at[u])
         sent(partner.at[u], hand_send.at[u])
 
         @pl.when(inner)
         def _():
-            sent(wa.at[pl.ds(0, 5)], ga_send.at[u])
-            sent(wb.at[pl.ds(0, 10)], gb_send.at[u])
+            sent(w_own.at[pl.ds(0, 5), pl.ds(0, GA)], ga_send.at[u])
+            sent(w_own.at[pl.ds(0, 10), pl.ds(GA, GB)], gb_send.at[u])
 
         @pl.when(jnp.logical_not(inner))
         def _():
-            sent(wa.at[0], ga_send.at[u])
-            sent(wb.at[pl.ds(0, 2)], gb_send.at[u])
+            sent(w_own.at[0, pl.ds(0, GA)], ga_send.at[u])
+            sent(w_own.at[pl.ds(0, 2), pl.ds(GA, GB)], gb_send.at[u])
 
         arrived(partner.at[u], hand_recv.at[u])
         return 0
@@ -501,10 +501,9 @@
                 pltpu.VMEM((2, 4, A, LANES), BF16),
                 pltpu.VMEM((3, 4, A, LANES), BF16),
                 pltpu.VMEM((2, 2, 4, B, LANES), BF16),
-                pltpu.VMEM((UNITS, A, LANES), BF16),
-                pltpu.VMEM((UNITS, B, LANES), BF16),
+                pltpu.VMEM((UNITS, ROWS, LANES), BF16),
                 *(by_unit, by_unit),
-                *(dma((2,)), dma((3,)), dma((2,)), *(dma((3,)),) * 3, by_unit, by_unit),
+                *(dma((2,)), dma((3,)), dma((2,)), *(dma((3,)),) * 2, by_unit, by_unit),
                 *(by_unit,) * 4,
                 *(by_unit, dma((UNITS, 2, 3)), by_unit, dma((UNITS, 2, 3))),
                 *(by_unit, dma((UNITS, 2, 3)), by_unit, dma((UNITS, 2, 3, 2))),

time: 591 us -> 585 us (0.990)
  Pallas kernels: 590 us -> 584 us
where the time goes in v4:
time: 585 us
  Pallas kernels  584 us (100%)
    pallas_call x1, Pallas kernels, step(): pl.pallas_call(kernel, out_shape=(*hbm[:2], *kept, jax.ShapeDtypeStruct((...  544 us
    pallas_call x1, Pallas kernels, step(): pl.pallas_call(unload, out_shape=(*hbm, *(jax.ShapeDtypeStruct(a.shape, a...  39.5 us

profile of v4, /device:TPU:0, one launch (start us, length us, event | category | flops | bytes accessed | tf_op | source)
XLA Modules:
  0.0 584.7 jit_solution(4895185169836140473)
XLA Ops:
  0.6 544.5 %shard_map.187 = (bf16[2,2,4,2,72,4608]{5,4,3,2,1,0:T(8,128)(2,1)}, bf16[2,2,4,2,72,4608]{5,4,3,2,1,0:T(8,128)(2,1)}, bf16[2,2,4,2,4,72,1152]{6,5,4,3,2,1,0:T(8,...) custom-call(bf16[2,2,4,2,72,4608]{5,4,3,2,1,0:T(8,128)(2,1)} %bitcas, ...), custom_call_target="tpu_custom_call" | custom-call | tf_op jit(solution)/shard_map/pallas_call | solution.py:483
  545.1 39.5 %shard_map.188 = (bf16[2,2,4,2,72,4608]{5,4,3,2,1,0:T(8,128)(2,1)}, bf16[2,2,4,2,72,4608]{5,4,3,2,1,0:T(8,128)(2,1)}, bf16[2,2,4,2,4,72,1152]{6,5,4,3,2,1,0:T(8,...) custom-call(bf16[2,2,4,2,72,4608]{5,4,3,2,1,0:T(8,128)(2,1)} %get-tu, ...), custom_call_target="tpu_custom_call" | custom-call | tf_op jit(solution)/shard_map/pallas_call | solution.py:514

commit v5 on v4

--- a/solution.py
+++ b/solution.py
@@ -8,7 +8,7 @@
 F32, BF16 = jnp.float32, jnp.bfloat16
 MESH = pl.DeviceIdType.MESH
 UNITS = 24
-RING, SLOTS = 4, 5
+RING, SLOTS = 4, 8
 ROWS, A, B, LANES = 72, 40, 32, 1152
 GA, GB = 48, 24
 LAG, B_STEP, B_OWN, B_OTHER, HAND, B_FIRST = 2, 4, 4, 5, 10, False
@@ -387,12 +387,12 @@
 
     early = [(LAG + f, hops_a, f) for f in range(3)] + [(f, hops_b, f) for f in range(3)]
     early = early[::-1] if B_FIRST else early
-    early += [(LAG + 3 + k, relays_a, k) for k in range(1, 4)]
     early += [(LAG + 3, step_a), (3, line_b)]
     middle = [(LAG - 8 + b, sum_t, b) for b in range(4)]
     middle += [(-4, sum_b, 0, 2), (-3, sum_b, 2, 2), (LAG - 1, sum_a, 0, 4)]
     middle += [(-16, to_partner), (LAG - 9, load_t), (-7, load_b), (LAG - 2, load_a), (1, load_state), (8, free_x), (3, free_y)]
     late = [(B_OWN + k, relays_b, k, 0) for k in range(1, 4)] + [(B_OTHER + k, relays_b, k, 1) for k in range(1, 4)]
+    late = [(LAG + 3 + k, relays_a, k) for k in range(1, 4)] + late
     late += [(B_STEP, step_b)] + ([(B_OWN, own_b_out)] if B_OWN != B_STEP else []) + [(B_OTHER, from_across_b), (HAND, hand_over)]
 
     to_partner(0)
@@ -448,15 +448,16 @@
 
     for n in range(SLOTS):
         read(n).start()
-    pltpu.make_async_copy(down, new_w[2], down_sem).start()
-    for u in range(UNITS):
-        which, layer, q = u // 8, u // 4 % 2, u % 4
-        for i, to in enumerate((new_m, new_v)):
-            target = to[which].at[layer, q] if which == 2 else to[which].at[layer, :, pl.ds(q * LANES, LANES)]
-            pltpu.make_async_copy(mv.at[u, i], target, mv_sem).start()
     for n in range(len(chunks)):
         read(n).wait()
         write(n).start()
+        if n == 5:
+            pltpu.make_async_copy(down, new_w[2], down_sem).start()
+            for u in range(UNITS):
+                which, layer, q = u // 8, u // 4 % 2, u % 4
+                for i, to in enumerate((new_m, new_v)):
+                    target = to[which].at[layer, q] if which == 2 else to[which].at[layer, :, pl.ds(q * LANES, LANES)]
+                    pltpu.make_async_copy(mv.at[u, i], target, mv_sem).start()
         ahead = n + SLOTS - 2
         if n >= 2 and ahead < len(chunks):
             write(ahead - SLOTS).wait()

time: 585 us -> 582 us (level)
  no operation moved by 1% of the time
where the time goes in v5:
time: 582 us; the launch traced here: 581 us
  Pallas kernels  580 us (100%)
    pallas_call x1, Pallas kernels, step(): pl.pallas_call(kernel, out_shape=(*hbm[:2], *kept, jax.ShapeDtypeStruct((...  542 us
    pallas_call x1, Pallas kernels, step(): pl.pallas_call(unload, out_shape=(*hbm, *(jax.ShapeDtypeStruct(a.shape, a...  38.8 us

profile of v5, /device:TPU:0, one launch (start us, length us, event | category | flops | bytes accessed | tf_op | source)
XLA Modules:
  0.0 581.1 jit_solution(2924686632027119755)
XLA Ops:
  0.6 541.7 %shard_map.187 = (bf16[2,2,4,2,72,4608]{5,4,3,2,1,0:T(8,128)(2,1)}, bf16[2,2,4,2,72,4608]{5,4,3,2,1,0:T(8,128)(2,1)}, bf16[2,2,4,2,4,72,1152]{6,5,4,3,2,1,0:T(8,...) custom-call(bf16[2,2,4,2,72,4608]{5,4,3,2,1,0:T(8,128)(2,1)} %bitcas, ...), custom_call_target="tpu_custom_call" | custom-call | tf_op jit(solution)/shard_map/pallas_call | solution.py:484
  542.3 38.8 %shard_map.188 = (bf16[2,2,4,2,72,4608]{5,4,3,2,1,0:T(8,128)(2,1)}, bf16[2,2,4,2,72,4608]{5,4,3,2,1,0:T(8,128)(2,1)}, bf16[2,2,4,2,4,72,1152]{6,5,4,3,2,1,0:T(8,...) custom-call(bf16[2,2,4,2,72,4608]{5,4,3,2,1,0:T(8,128)(2,1)} %get-tu, ...), custom_call_target="tpu_custom_call" | custom-call | tf_op jit(solution)/shard_map/pallas_call | solution.py:515
